TPU v7x, 256 devices: a whole 4x4x8 slice. The times are simulated.
256 devices in a mesh: layer: 16 (over y, x_hi, core), feat: 16 (over z, x_lo).
Axes of the slice: x: 4 (x_hi: 2, x_lo: 2; x = x_hi * 2 + x_lo), y: 4, z: 8, core: 2. Of those that a mesh axis runs over, the one named last changes fastest.
Arguments:
- residual_in: bfloat16 [16, 256, 4096], P('layer', None, 'feat'), may hold values from -6 to 6
- mlp_out: bfloat16 [16, 256, 4096], P('layer', None, 'feat'), may hold values from -6 to 6
- encoder: bfloat16 [16, 4096, 2048], P('layer', None, 'feat'), may hold values from -0.09375 to 0.09375
- encoder_bias: float32 [16, 2048], P('layer', 'feat'), may hold values from -3 to 3
- decoder: bfloat16 [16, 9, 2048, 4096], P('layer', None, 'feat'), may hold values from -0.046875 to 0.046875
- decoder_bias: float32 [16, 4096], P('layer'), may hold values from -3 to 3
Outputs:
- recon_error: bfloat16 [16, 256, 4096], P('layer', None, 'feat')
- pre_grad: float32 [16, 256, 2048], P('layer', None, 'feat')
All inputs are finite; a program needn't handle non-finite values.
Results may differ from a plain program's by a relative error of at most 0.0035.
Values may be sent and summed in bfloat16 or wider, within the bound.
A program may use at most 128 MiB of HBM per device.

v0:
```python
import jax
import jax.numpy as jnp
from jax import lax
from jax.sharding import Mesh
from jax.sharding import PartitionSpec as P

FEAT = ("feat_0", "feat_1")


def sent_to_all(array, axis):
    copies = jnp.broadcast_to(array, (lax.axis_size(axis), *array.shape))
    return lax.all_to_all(copies, axis, split_axis=0, concat_axis=0, tiled=True)


def joined_along(blocks, dim):
    shape = list(blocks.shape[1:])
    shape[dim] *= blocks.shape[0]
    return jnp.moveaxis(blocks, 0, dim).reshape(shape)


def collect(array, axis, dim):
    blocks = sent_to_all(array, axis)
    return joined_along(blocks, dim)


def scatter_axes(array, axes, dim):
    for axis in axes:
        array = lax.psum_scatter(array, axis, scatter_dimension=dim, tiled=True)
    return array


def swapped(array, axis, bit):
    return lax.ppermute(array, axis, [(i, i ^ 1 << bit) for i in range(lax.axis_size(axis))])


def sent_together(arrays, axis, dim, along):
    both = jnp.concatenate(arrays, axis=along)
    whole, at, outs = (lax.all_gather(both, axis, axis=dim, tiled=True), 0, [])
    for a in arrays:
        outs.append(lax.slice_in_dim(whole, at, at + a.shape[along], axis=along))
        at += a.shape[along]
    return tuple(outs)


def in_blocks(array, dim, peers):
    before, after = (array.shape[:dim], array.shape[dim + 1 :])
    return jnp.moveaxis(array.reshape(*before, peers, -1, *after), dim, 0)


def sum_at_owner(array, axis, dim):
    peers = lax.axis_size(axis)
    blocks = lax.all_to_all(in_blocks(array, dim, peers), axis, 0, 0, tiled=True)
    return jnp.sum(blocks, axis=0)


def placement_of(source, layer_row, half_layers, layers):
    own_flag = source <= jnp.minimum(layer_row, half_layers - 1)
    slot_index = jnp.where(own_flag, source, source - half_layers + layer_row + 1)
    over_flag = (
        jnp.logical_not(own_flag) & (source >= half_layers) & (source <= layers - 1 - layer_row)
    )
    return (slot_index, own_flag, over_flag)


def add_source(carry, code_rows, source, layer_row, half_layers, layers, weights):
    slot_index, own_flag, over_flag = placement_of(source, layer_row, half_layers, layers)

    def compute(inner):
        picked = jnp.clip(slot_index, 0, weights.shape[0] - 1)
        block = lax.dynamic_index_in_dim(weights, picked, 0, keepdims=False)
        product = jnp.dot(code_rows, block, preferred_element_type=jnp.float32)
        return (
            inner[0] + jnp.where(own_flag, product, 0.0),
            inner[1] + jnp.where(over_flag, product, 0.0),
        )

    def unchanged(inner):
        return inner

    return lax.cond(own_flag | over_flag, compute, unchanged, carry)


def shards(residual_in, mlp_out, encoder, encoder_bias, decoder, decoder_bias):
    layer_row = lax.axis_index("layer")
    layers = lax.axis_size("layer")
    half_layers = layers // 2
    weights = decoder[0]
    slot_count = weights.shape[0]
    enc_local = encoder[0]
    tokens = residual_in.shape[1]
    model_width = weights.shape[2]
    preact = jnp.dot(
        lax.all_gather(residual_in[0], FEAT, axis=1, tiled=True),
        enc_local,
        preferred_element_type=jnp.float32,
    )
    preact = preact + encoder_bias[0][None, :]
    codes = jnp.maximum(preact, 0.0).astype(jnp.bfloat16)
    empty = jnp.zeros((tokens, model_width), jnp.float32)
    piece = collect(codes[None], "layer", 0)

    def one_row(offset, inner):
        code_rows = lax.dynamic_index_in_dim(piece, offset, 0, keepdims=False)
        return add_source(inner, code_rows, offset, layer_row, half_layers, layers, weights)

    own_part, over_part = lax.fori_loop(0, piece.shape[0], one_row, (empty, empty))
    own_sum, over_sum = (scatter_axes(own_part, FEAT, 1), scatter_axes(over_part, FEAT, 1))
    hops = layers.bit_length() - 1
    for bit in range(hops):
        over_sum = swapped(over_sum, "layer", bit)
    column = lax.axis_index(FEAT)
    share_width = model_width // lax.axis_size(FEAT)
    bias_share = lax.dynamic_slice_in_dim(decoder_bias[0], column * share_width, share_width, 0)
    target_share = mlp_out[0].astype(jnp.float32)
    error_share = (own_sum + over_sum + bias_share[None, :] - target_share).astype(jnp.bfloat16)
    partner_share = error_share
    for bit in range(hops):
        partner_share = swapped(partner_share, "layer", bit)
    error_full, partner_full = sent_together((error_share, partner_share), FEAT, 1, 0)
    slot_ids = jnp.arange(slot_count, dtype=jnp.int32)
    own_slot = slot_ids <= jnp.minimum(layer_row, half_layers - 1)
    slot_errors = jnp.where(own_slot[:, None, None], error_full[None], partner_full[None])
    slot_terms = jnp.einsum(
        "jtd,jfd->jtf", slot_errors, weights, preferred_element_type=jnp.float32
    )
    sources = jnp.arange(layers, dtype=jnp.int32)
    slot_index, own_flag, over_flag = placement_of(sources, layer_row, half_layers, layers)
    picked = jnp.take(slot_terms, jnp.clip(slot_index, 0, slot_count - 1), axis=0)
    by_source = jnp.where((own_flag | over_flag)[:, None, None], picked, 0.0)
    back = sum_at_owner(by_source, "layer", 0)
    return (error_share[None], back)


def solution(mesh):
    split = Mesh(mesh.devices.reshape(mesh.shape["layer"], 8, 2), ("layer", "feat_0", "feat_1"))
    placed = (
        P("layer", None, FEAT),
        P("layer", None, FEAT),
        P("layer", None, FEAT),
        P("layer", FEAT),
        P("layer", None, FEAT, None),
        P("layer", None),
    )
    return jax.shard_map(
        shards,
        mesh=split,
        in_specs=placed,
        out_specs=(P("layer", None, FEAT), P("layer", None, FEAT)),
        check_vma=False,
    )
```

profile of v0, /device:TPU:2, one launch (start us, length us, event | category | flops | bytes accessed | tf_op | source)
XLA Modules:
  0.0 552.4 jit_solution(7001553876224597050)
XLA Ops:
  7.9 84.9 %all-gather.6.cloned.1.call-done = bf16[1,256,4096]{2,1,0:T(8,128)(2,1)} async-done(((bf16[1,256,256]{2,1,0:T(8,128)(2,1)}), bf16[1,256,4096]{2,1,0:T(8,128)(2,1)}) %all-gather.6.cloned.1.call-update) | async-done | bytes 2097168 | tf_op jit(solution)/shard_map/all_gather | solution.py:93
  104.1 18.0 %all-to-all-done = bf16[16,1,256,128]{3,2,1,0:T(8,128)(2,1)S(1)} async-done(((bf16[16,1,256,128]{3,2,1,0:T(8,128)(2,1)}), bf16[16,1,256,128]{3,2,1,0:T(8,128)(2,1)S(1)}, u32[]{:S(2)}, u32[]{:S(2)}) %all-to-all-start) | async-done | bytes 1048608 | tf_op jit(solution)/shard_map/all_to_all | solution.py:12
  127.0 70.8 %while.17 = (s32[]{:T(128)}, f32[256,4096]{1,0:T(8,128)}, f32[256,4096]{1,0:T(8,128)}, s32[]{:T(128)}, s32[]{:T(128)}, /*index=5*/bf16[16,256,128]{2,1,0:T(8,128...) while((s32[]{:T(128)}, f32[256,4096]{1,0:T(8,128)}, f32[256,4096]{1,0:T(8,128)}, ...), condition=%wide.region_3.4_spmd, body=%wide.region_0.3_spmd.sunk | while | flops 272629760 | bytes 17892716 | solution.py:106
  127.0 7.9 %conditional.2 = ((f32[256,4096]{1,0:T(8,128)}, f32[256,4096]{1,0:T(8,128)})) conditional(s32[]{:T(128)} %convert_element_type.30, (f32[256,4096]{1,0:T(8,128)}, f32[256,4096]{1,0:T(8,128)}) %tuple.62, (pred[]{:T(512)}, s32[]{:T(128)}, bf16[16,256,128]{2,1,0:T(8,128)(2,1)S(1)}, s32[]{:T(128)}, bf16[9,128,4096]{2,1,0:T(8,128)(2,1)}, ...), branch_computations={%region_1.1_spmd, %region_2.2_spmd} | conditional | flops 272629760 | bytes 17892492 | solution.py:80
  127.0 7.9 %select_add_fusion = (f32[256,4096]{1,0:T(8,128)}, f32[256,4096]{1,0:T(8,128)}) fusion(f32[256,4096]{1,0:T(8,128)} %get-tuple-element.269, pred[]{:T(512)} %get-tuple-element.270, f32[256,4096]{1,0:T(8,128)} %get-tuple-element.263, pred[]{:T(512)} %get-tuple-element.264, bf16[9,128,4096]{2,1,0:T(8,128)(2,1)} %get-tuple-element.267, s32[]{:T(128)S(6)} %min.21, ...), kind=kOutput, calls=%fused_computation.1 | convolution fusion | flops 272629760 | bytes 17892360 | tf_op jit(solution)/shard_map/while/body/eval_jaxpr/cond/branch_1_fun/dot_general | solution.py:71
  134.9 7.9 %conditional.2 = ((f32[256,4096]{1,0:T(8,128)}, f32[256,4096]{1,0:T(8,128)})) conditional(s32[]{:T(128)} %convert_element_type.30, (f32[256,4096]{1,0:T(8,128)}, f32[256,4096]{1,0:T(8,128)}) %tuple.62, (pred[]{:T(512)}, s32[]{:T(128)}, bf16[16,256,128]{2,1,0:T(8,128)(2,1)S(1)}, s32[]{:T(128)}, bf16[9,128,4096]{2,1,0:T(8,128)(2,1)}, ...), branch_computations={%region_1.1_spmd, %region_2.2_spmd} | conditional | flops 272629760 | bytes 17892492 | solution.py:80
  135.0 7.9 %select_add_fusion = (f32[256,4096]{1,0:T(8,128)}, f32[256,4096]{1,0:T(8,128)}) fusion(f32[256,4096]{1,0:T(8,128)} %get-tuple-element.269, pred[]{:T(512)} %get-tuple-element.270, f32[256,4096]{1,0:T(8,128)} %get-tuple-element.263, pred[]{:T(512)} %get-tuple-element.264, bf16[9,128,4096]{2,1,0:T(8,128)(2,1)} %get-tuple-element.267, s32[]{:T(128)S(6)} %min.21, ...), kind=kOutput, calls=%fused_computation.1 | convolution fusion | flops 272629760 | bytes 17892360 | tf_op jit(solution)/shard_map/while/body/eval_jaxpr/cond/branch_1_fun/dot_general | solution.py:71
  142.8 7.9 %conditional.2 = ((f32[256,4096]{1,0:T(8,128)}, f32[256,4096]{1,0:T(8,128)})) conditional(s32[]{:T(128)} %convert_element_type.30, (f32[256,4096]{1,0:T(8,128)}, f32[256,4096]{1,0:T(8,128)}) %tuple.62, (pred[]{:T(512)}, s32[]{:T(128)}, bf16[16,256,128]{2,1,0:T(8,128)(2,1)S(1)}, s32[]{:T(128)}, bf16[9,128,4096]{2,1,0:T(8,128)(2,1)}, ...), branch_computations={%region_1.1_spmd, %region_2.2_spmd} | conditional | flops 272629760 | bytes 17892492 | solution.py:80
  142.8 7.8 %select_add_fusion = (f32[256,4096]{1,0:T(8,128)}, f32[256,4096]{1,0:T(8,128)}) fusion(f32[256,4096]{1,0:T(8,128)} %get-tuple-element.269, pred[]{:T(512)} %get-tuple-element.270, f32[256,4096]{1,0:T(8,128)} %get-tuple-element.263, pred[]{:T(512)} %get-tuple-element.264, bf16[9,128,4096]{2,1,0:T(8,128)(2,1)} %get-tuple-element.267, s32[]{:T(128)S(6)} %min.21, ...), kind=kOutput, calls=%fused_computation.1 | convolution fusion | flops 272629760 | bytes 17892360 | tf_op jit(solution)/shard_map/while/body/eval_jaxpr/cond/branch_1_fun/dot_general | solution.py:71
  150.7 7.9 %conditional.2 = ((f32[256,4096]{1,0:T(8,128)}, f32[256,4096]{1,0:T(8,128)})) conditional(s32[]{:T(128)} %convert_element_type.30, (f32[256,4096]{1,0:T(8,128)}, f32[256,4096]{1,0:T(8,128)}) %tuple.62, (pred[]{:T(512)}, s32[]{:T(128)}, bf16[16,256,128]{2,1,0:T(8,128)(2,1)S(1)}, s32[]{:T(128)}, bf16[9,128,4096]{2,1,0:T(8,128)(2,1)}, ...), branch_computations={%region_1.1_spmd, %region_2.2_spmd} | conditional | flops 272629760 | bytes 17892492 | solution.py:80
  150.7 7.9 %select_add_fusion = (f32[256,4096]{1,0:T(8,128)}, f32[256,4096]{1,0:T(8,128)}) fusion(f32[256,4096]{1,0:T(8,128)} %get-tuple-element.269, pred[]{:T(512)} %get-tuple-element.270, f32[256,4096]{1,0:T(8,128)} %get-tuple-element.263, pred[]{:T(512)} %get-tuple-element.264, bf16[9,128,4096]{2,1,0:T(8,128)(2,1)} %get-tuple-element.267, s32[]{:T(128)S(6)} %min.21, ...), kind=kOutput, calls=%fused_computation.1 | convolution fusion | flops 272629760 | bytes 17892360 | tf_op jit(solution)/shard_map/while/body/eval_jaxpr/cond/branch_1_fun/dot_general | solution.py:71
  158.5 7.9 %conditional.2 = ((f32[256,4096]{1,0:T(8,128)}, f32[256,4096]{1,0:T(8,128)})) conditional(s32[]{:T(128)} %convert_element_type.30, (f32[256,4096]{1,0:T(8,128)}, f32[256,4096]{1,0:T(8,128)}) %tuple.62, (pred[]{:T(512)}, s32[]{:T(128)}, bf16[16,256,128]{2,1,0:T(8,128)(2,1)S(1)}, s32[]{:T(128)}, bf16[9,128,4096]{2,1,0:T(8,128)(2,1)}, ...), branch_computations={%region_1.1_spmd, %region_2.2_spmd} | conditional | flops 272629760 | bytes 17892492 | solution.py:80
  166.4 7.9 %conditional.2 = ((f32[256,4096]{1,0:T(8,128)}, f32[256,4096]{1,0:T(8,128)})) conditional(s32[]{:T(128)} %convert_element_type.30, (f32[256,4096]{1,0:T(8,128)}, f32[256,4096]{1,0:T(8,128)}) %tuple.62, (pred[]{:T(512)}, s32[]{:T(128)}, bf16[16,256,128]{2,1,0:T(8,128)(2,1)S(1)}, s32[]{:T(128)}, bf16[9,128,4096]{2,1,0:T(8,128)(2,1)}, ...), branch_computations={%region_1.1_spmd, %region_2.2_spmd} | conditional | flops 272629760 | bytes 17892492 | solution.py:80
  166.4 7.9 %select_add_fusion = (f32[256,4096]{1,0:T(8,128)}, f32[256,4096]{1,0:T(8,128)}) fusion(f32[256,4096]{1,0:T(8,128)} %get-tuple-element.269, pred[]{:T(512)} %get-tuple-element.270, f32[256,4096]{1,0:T(8,128)} %get-tuple-element.263, pred[]{:T(512)} %get-tuple-element.264, bf16[9,128,4096]{2,1,0:T(8,128)(2,1)} %get-tuple-element.267, s32[]{:T(128)S(6)} %min.21, ...), kind=kOutput, calls=%fused_computation.1 | convolution fusion | flops 272629760 | bytes 17892360 | tf_op jit(solution)/shard_map/while/body/eval_jaxpr/cond/branch_1_fun/dot_general | solution.py:71
  174.2 7.9 %conditional.2 = ((f32[256,4096]{1,0:T(8,128)}, f32[256,4096]{1,0:T(8,128)})) conditional(s32[]{:T(128)} %convert_element_type.30, (f32[256,4096]{1,0:T(8,128)}, f32[256,4096]{1,0:T(8,128)}) %tuple.62, (pred[]{:T(512)}, s32[]{:T(128)}, bf16[16,256,128]{2,1,0:T(8,128)(2,1)S(1)}, s32[]{:T(128)}, bf16[9,128,4096]{2,1,0:T(8,128)(2,1)}, ...), branch_computations={%region_1.1_spmd, %region_2.2_spmd} | conditional | flops 272629760 | bytes 17892492 | solution.py:80
  182.1 7.9 %conditional.2 = ((f32[256,4096]{1,0:T(8,128)}, f32[256,4096]{1,0:T(8,128)})) conditional(s32[]{:T(128)} %convert_element_type.30, (f32[256,4096]{1,0:T(8,128)}, f32[256,4096]{1,0:T(8,128)}) %tuple.62, (pred[]{:T(512)}, s32[]{:T(128)}, bf16[16,256,128]{2,1,0:T(8,128)(2,1)S(1)}, s32[]{:T(128)}, bf16[9,128,4096]{2,1,0:T(8,128)(2,1)}, ...), branch_computations={%region_1.1_spmd, %region_2.2_spmd} | conditional | flops 272629760 | bytes 17892492 | solution.py:80
  182.1 7.9 %select_add_fusion = (f32[256,4096]{1,0:T(8,128)}, f32[256,4096]{1,0:T(8,128)}) fusion(f32[256,4096]{1,0:T(8,128)} %get-tuple-element.269, pred[]{:T(512)} %get-tuple-element.270, f32[256,4096]{1,0:T(8,128)} %get-tuple-element.263, pred[]{:T(512)} %get-tuple-element.264, bf16[9,128,4096]{2,1,0:T(8,128)(2,1)} %get-tuple-element.267, s32[]{:T(128)S(6)} %min.21, ...), kind=kOutput, calls=%fused_computation.1 | convolution fusion | flops 272629760 | bytes 17892360 | tf_op jit(solution)/shard_map/while/body/eval_jaxpr/cond/branch_1_fun/dot_general | solution.py:71
  189.9 7.9 %conditional.2 = ((f32[256,4096]{1,0:T(8,128)}, f32[256,4096]{1,0:T(8,128)})) conditional(s32[]{:T(128)} %convert_element_type.30, (f32[256,4096]{1,0:T(8,128)}, f32[256,4096]{1,0:T(8,128)}) %tuple.62, (pred[]{:T(512)}, s32[]{:T(128)}, bf16[16,256,128]{2,1,0:T(8,128)(2,1)S(1)}, s32[]{:T(128)}, bf16[9,128,4096]{2,1,0:T(8,128)(2,1)}, ...), branch_computations={%region_1.1_spmd, %region_2.2_spmd} | conditional | flops 272629760 | bytes 17892492 | solution.py:80
  197.9 51.0 %reduce-scatter.9.cloned.1.call-done = f32[256,512]{1,0:T(8,128)} async-done(((f32[256,4096]{1,0:T(8,128)}), f32[256,512]{1,0:T(8,128)}) %reduce-scatter.9.cloned.1.call-update) | async-done | bytes 524304 | tf_op jit(solution)/shard_map/reduce_scatter | solution.py:28
  249.5 19.1 %reduce-scatter.11.cloned.1.call-done = f32[256,256]{1,0:T(8,128)} async-done(((f32[256,512]{1,0:T(8,128)}), f32[256,256]{1,0:T(8,128)}) %reduce-scatter.11.cloned.1.call-update) | async-done | bytes 262160 | tf_op jit(solution)/shard_map/reduce_scatter | solution.py:28
  268.7 59.9 %reduce-scatter.5.cloned.1.call-done = f32[256,512]{1,0:T(8,128)} async-done(((f32[256,4096]{1,0:T(8,128)}), f32[256,512]{1,0:T(8,128)}) %reduce-scatter.5.cloned.1.call-update) | async-done | bytes 524304 | tf_op jit(solution)/shard_map/reduce_scatter | solution.py:28
  375.0 118.1 %all-gather.4.cloned.1.call-done = bf16[512,4096]{1,0:T(8,128)(2,1)} async-done(((bf16[512,256]{1,0:T(8,128)(2,1)}), bf16[512,4096]{1,0:T(8,128)(2,1)}) %all-gather.4.cloned.1.call-update) | async-done | bytes 4194320 | tf_op jit(solution)/shard_map/all_gather | solution.py:38
  495.8 8.8 %fusion.6 = f32[9,256,128]{2,1,0:T(8,128)} fusion(pred[9]{0:T(512)(128)(4,1)S(1)} %iota_compare_fusion, bf16[256,4096]{1,0:T(8,128)(2,1)S(1)} %get-tuple-element.307, bf16[256,4096]{1,0:T(8,128)(2,1)S(1)} %get-tuple-element.306, bf16[1,9,128,4096]{3,2,1,0:T(8,128)(2,1)} %bitcast.44), kind=kOutput, calls=%fused_computation.9 | convolution fusion | flops 2425356288 | bytes 14811145 | tf_op jit(solution)/shard_map/jtd,jfd->jtf/dot_general | solution.py:123
  506.9 37.9 %all_to_all.10 = f32[16,1,256,128]{3,2,1,0:T(8,128)S(1)} all-to-all(f32[16,1,256,128]{3,2,1,0:T(8,128)S(1)} %fusion.12), channel_id=1, replica_groups=mesh['layer'=16,'feat_0'=8,'feat_1'=2] {'layer'}, dimensions={0} | all-to-all | bytes 4194304 | tf_op jit(solution)/shard_map/all_to_all | solution.py:52
  (61 shorter events, 93.2 us)
Async XLA Ops:
  7.2 85.6 %copy-start = (bf16[1,4096,128]{2,1,0:T(8,128)(2,1)S(1)}, bf16[1,4096,128]{2,1,0:T(8,128)(2,1)}, u32[]{:S(2)}) copy-start(bf16[1,4096,128]{2,1,0:T(8,128)(2,1)} %param.12) | copy-start | bytes 3145732
  7.2 85.6 %all-gather.6.cloned.1.call-start = ((), (), s32[]{:S(2)}) async-start(), calls=%async_computation.11 | async-start | bytes 2228224 | tf_op jit(solution)/shard_map/all_gather | solution.py:93
  96.3 25.8 %all-to-all-start = ((bf16[16,1,256,128]{3,2,1,0:T(8,128)(2,1)}), bf16[16,1,256,128]{3,2,1,0:T(8,128)(2,1)S(1)}, u32[]{:S(2)}, u32[]{:S(2)}) async-start(bf16[16,1,256,128]{3,2,1,0:T(8,128)(2,1)} %broadcast_in_dim.69), calls=%async_computation | async-start | bytes 2097152 | tf_op jit(solution)/shard_map/all_to_all | solution.py:12
  104.0 144.9 %reduce-scatter.9.cloned.1.call-start = ((), (), s32[]{:S(2)}) async-start(), calls=%async_computation.8 | async-start | bytes 4718592 | tf_op jit(solution)/shard_map/reduce_scatter | solution.py:28
  197.8 155.4 %copy-start.2 = (bf16[1,256,256]{2,1,0:T(8,128)(2,1)S(1)}, bf16[1,256,256]{2,1,0:T(8,128)(2,1)}, u32[]{:S(2)}) copy-start(bf16[1,256,256]{2,1,0:T(8,128)(2,1)} %param.11) | copy-start | bytes 393220
  197.8 70.9 %reduce-scatter.11.cloned.1.call-start = ((), (), s32[]{:S(2)}) async-start(), calls=%async_computation.9 | async-start | bytes 786432 | tf_op jit(solution)/shard_map/reduce_scatter | solution.py:28
  248.9 79.6 %reduce-scatter.5.cloned.1.call-start = ((), (), s32[]{:S(2)}) async-start(), calls=%async_computation.6 | async-start | bytes 4718592 | tf_op jit(solution)/shard_map/reduce_scatter | solution.py:28
  249.5 99.5 %reduce-scatter.7.cloned.1.call-start = ((), (), s32[]{:S(2)}) async-start(), calls=%async_computation.7 | async-start | bytes 786432 | tf_op jit(solution)/shard_map/reduce_scatter | solution.py:28
  268.7 59.9 %collective-permute-start = (f32[256,256]{1,0:T(8,128)}, f32[256,256]{1,0:T(8,128)S(1)}, u32[]{:S(2)}, u32[]{:S(2)}) collective-permute-start(f32[256,256]{1,0:T(8,128)} %reduce-scatter.11.cloned.1.call-done), channel_id=1, source_target_pairs={{0,16},{16,0},{32,48},{48,32},{64,80},{80,64},{96,112},{112,96},{1... | collective-permute-start | bytes 786440 | tf_op jit(solution)/shard_map/ppermute | solution.py:33
  328.6 164.5 %all-gather.4.cloned.1.call-start = ((), (), s32[]{:S(2)}) async-start(), calls=%async_computation.10 | async-start | bytes 4456448 | tf_op jit(solution)/shard_map/all_gather | solution.py:38
  328.6 9.6 %collective-permute-start.1 = (f32[256,256]{1,0:T(8,128)S(1)}, f32[256,256]{1,0:T(8,128)S(1)}, u32[]{:S(2)}, u32[]{:S(2)}) collective-permute-start(f32[256,256]{1,0:T(8,128)S(1)} %collective-permute-done), channel_id=1, source_target_pairs={{0,32},{16,48},{32,0},{48,16},{64,96},{80,112},{96,64},{112,80},{1... | collective-permute-start | bytes 786440 | tf_op jit(solution)/shard_map/ppermute | solution.py:33
  338.2 7.1 %collective-permute-start.2 = (f32[256,256]{1,0:T(8,128)S(1)}, f32[256,256]{1,0:T(8,128)S(1)}, u32[]{:S(2)}, u32[]{:S(2)}) collective-permute-start(f32[256,256]{1,0:T(8,128)S(1)} %collective-permute-done.1), channel_id=1, source_target_pairs={{0,64},{16,80},{32,96},{48,112},{64,0},{80,16},{96,32},{112,48},{1... | collective-permute-start | bytes 786440 | tf_op jit(solution)/shard_map/ppermute | solution.py:33
  345.3 7.9 %collective-permute-start.3 = (f32[256,256]{1,0:T(8,128)S(1)}, f32[256,256]{1,0:T(8,128)S(1)}, u32[]{:S(2)}, u32[]{:S(2)}) collective-permute-start(f32[256,256]{1,0:T(8,128)S(1)} %collective-permute-done.2), channel_id=1, source_target_pairs={{0,128},{16,144},{32,160},{48,176},{64,192},{80,208},{96,224},{112... | collective-permute-start | bytes 786440 | tf_op jit(solution)/shard_map/ppermute | solution.py:33
  354.2 141.6 %copy-start.1 = (bf16[256,256]{1,0:T(8,128)(2,1)}, bf16[256,256]{1,0:T(8,128)(2,1)S(1)}, u32[]{:S(2)}) copy-start(bf16[256,256]{1,0:T(8,128)(2,1)S(1)} %fusion.25) | copy-start | bytes 393220
  354.2 1.4 collective-permute-start.4
  355.6 7.1 %collective-permute-start.5 = (bf16[256,256]{1,0:T(8,128)(2,1)S(1)}, bf16[256,256]{1,0:T(8,128)(2,1)S(1)}, u32[]{:S(2)}, u32[]{:S(2)}) collective-permute-start(bf16[256,256]{1,0:T(8,128)(2,1)S(1)} %collective-permute-done.4), channel_id=1, source_target_pairs={{0,32},{16,48},{32,0},{48,16},{64,96},{80,112},{96,64},{112,80},{1... | collective-permute-start | bytes 393224 | tf_op jit(solution)/shard_map/ppermute | solution.py:33
  362.7 5.0 collective-permute-start.6
  367.7 6.5 %collective-permute-start.7 = (bf16[256,256]{1,0:T(8,128)(2,1)S(1)}, bf16[256,256]{1,0:T(8,128)(2,1)S(1)}, u32[]{:S(2)}, u32[]{:S(2)}) collective-permute-start(bf16[256,256]{1,0:T(8,128)(2,1)S(1)} %collective-permute-done.6), channel_id=1, source_target_pairs={{0,128},{16,144},{32,160},{48,176},{64,192},{80,208},{96,224},{112... | collective-permute-start | bytes 393224 | tf_op jit(solution)/shard_map/ppermute | solution.py:33
Sparse Core Ops, SparseCore 0:
  9.7 83.0 all-gather.5
  197.9 50.9 reduce-scatter.8
  251.4 17.2 reduce-scatter.10
  271.1 57.4 reduce-scatter.4
  330.9 17.2 reduce-scatter.6
  375.0 118.0 all-gather.3
where the time goes:
time: 553 us; the launch traced here: 552 us
  waiting for transfers between devices  383 us (69%)
  matrix products  81.8 us (15%)
  blocking collectives  37.9 us (7%)
  starting transfers between devices  21.3 us (4%)
  between operations  14.2 us (3%)
  local copies, waits for them, and re-layouts  11.5 us (2%)
    reduce_scatter x4, waiting for transfers between devices, scatter_axes(): array = lax.psum_scatter(array, axis, scatter_dimension=dim, tiled=True)  130 us
    all_gather x1, waiting for transfers between devices, sent_together(): whole, at, outs = (lax.all_gather(both, axis, axis=dim, tiled=True), 0, [])  118 us
    all_gather x1, waiting for transfers between devices, shards(): lax.all_gather(residual_in[0], FEAT, axis=1, tiled=True)  84.9 us
    dot_general x9, matrix products, compute(): product = jnp.dot(code_rows, block, preferred_element_type=jnp.float32)  70.7 us
    all_to_all x1, blocking collectives, sum_at_owner(): lax.all_to_all(in_blocks(array, dim, peers), axis, 0, 0, tiled=True)  37.9 us
    ppermute x8, waiting for transfers between devices, swapped(): lax.ppermute(array, axis, [(i, i ^ 1 << bit) for i in range(lax.axis_size...  30.5 us
    all_to_all x1, waiting for transfers between devices, sent_to_all(): return lax.all_to_all(copies, axis, split_axis=0, concat_axis=0, tiled=True)  18 us
    ppermute x8, starting transfers between devices, swapped(): lax.ppermute(array, axis, [(i, i ^ 1 << bit) for i in range(lax.axis_size...  13.3 us
  transfers between devices with their start and end apart: 15, of which 13 were waited for; matrix products, arithmetic and copies ran while one was open for 0% of the time, Pallas kernels for 0%

commit v1 on v0

--- a/solution.py
+++ b/solution.py
@@ -5,6 +5,13 @@
 from jax.sharding import PartitionSpec as P
 
 FEAT = ("feat_0", "feat_1")
+
+
+def gather_over(x, axis, dim):
+    size = lax.axis_size(axis)
+    tiles = jnp.stack([x for _ in range(size)])
+    tiles = lax.all_to_all(tiles, axis, split_axis=0, concat_axis=0)
+    return jnp.concatenate(tiles, axis=dim)
 
 
 def sent_to_all(array, axis):
@@ -90,9 +97,7 @@
     tokens = residual_in.shape[1]
     model_width = weights.shape[2]
     preact = jnp.dot(
-        lax.all_gather(residual_in[0], FEAT, axis=1, tiled=True),
-        enc_local,
-        preferred_element_type=jnp.float32,
+        gather_over(residual_in[0], FEAT, 1), enc_local, preferred_element_type=jnp.float32
     )
     preact = preact + encoder_bias[0][None, :]
     codes = jnp.maximum(preact, 0.0).astype(jnp.bfloat16)

time: 553 us -> 523 us (0.946)
  waiting for transfers between devices: 383 us -> 296 us
  blocking collectives: 37.9 us -> 96.6 us
    all_gather x1 -> x0, waiting for transfers between devices: 84.9 us -> none  [shards(): lax.all_gather(residual_in[0], FEAT, axis=1, tiled=True)]
    all_to_all x0 -> x1, blocking collectives: none -> 58.7 us  [gather_over(): tiles = lax.all_to_all(tiles, axis, split_axis=0, concat_axis=0)]
  transfers between devices with their start and end apart: 15 -> 14, of which waited for: 13 -> 12; matrix products, arithmetic and copies ran while one was open for 0% -> 0% of each run, Pallas kernels for 0% -> 0%
where the time goes in v1:
time: 523 us; the launch traced here: 522 us
  waiting for transfers between devices  296 us (57%)
  blocking collectives  96.6 us (18%)
  matrix products  80 us (15%)
  starting transfers between devices  19.7 us (4%)
  between operations  13.9 us (3%)
  local copies, waits for them, and re-layouts  12.7 us (2%)
    reduce_scatter x4, waiting for transfers between devices, scatter_axes(): array = lax.psum_scatter(array, axis, scatter_dimension=dim, tiled=True)  129 us
    all_gather x1, waiting for transfers between devices, sent_together(): whole, at, outs = (lax.all_gather(both, axis, axis=dim, tiled=True), 0, [])  118 us
    dot_general x9, matrix products, compute(): product = jnp.dot(code_rows, block, preferred_element_type=jnp.float32)  70.4 us
    all_to_all x1, blocking collectives, gather_over(): tiles = lax.all_to_all(tiles, axis, split_axis=0, concat_axis=0)  58.7 us
    all_to_all x1, blocking collectives, sum_at_owner(): lax.all_to_all(in_blocks(array, dim, peers), axis, 0, 0, tiled=True)  37.9 us
    ppermute x8, waiting for transfers between devices, swapped(): lax.ppermute(array, axis, [(i, i ^ 1 << bit) for i in range(lax.axis_size...  30.5 us
    all_to_all x1, waiting for transfers between devices, sent_to_all(): return lax.all_to_all(copies, axis, split_axis=0, concat_axis=0, tiled=True)  18 us
    ppermute x8, starting transfers between devices, swapped(): lax.ppermute(array, axis, [(i, i ^ 1 << bit) for i in range(lax.axis_size...  13.3 us
  transfers between devices with their start and end apart: 14, of which 12 were waited for; matrix products, arithmetic and copies ran while one was open for 0% of the time, Pallas kernels for 0%

profile of v1, /device:TPU:2, one launch (start us, length us, event | category | flops | bytes accessed | tf_op | source)
XLA Modules:
  0.0 522.1 jit_solution(14417106080039029459)
XLA Ops:
  8.5 58.7 %all_to_all.15 = bf16[16,256,256]{1,2,0:T(8,128)(2,1)S(1)} all-to-all(bf16[16,256,256]{1,2,0:T(8,128)(2,1)S(1)} %stack.3), channel_id=1, replica_groups=mesh['layer'=16,'feat_0'=8,'feat_1'=2] {'feat_0','feat_1'}, dimensions={0} | all-to-all | bytes 4194304 | tf_op jit(solution)/shard_map/all_to_all | solution.py:13
  75.3 18.0 %all-to-all-done.1 = bf16[16,1,256,128]{3,2,1,0:T(8,128)(2,1)S(1)} async-done(((bf16[16,1,256,128]{3,2,1,0:T(8,128)(2,1)}), bf16[16,1,256,128]{3,2,1,0:T(8,128)(2,1)S(1)}, u32[]{:S(2)}, u32[]{:S(2)}) %all-to-all-start.1) | async-done | bytes 1048608 | tf_op jit(solution)/shard_map/all_to_all | solution.py:19
  98.2 70.6 %while.17 = (s32[]{:T(128)}, f32[256,4096]{1,0:T(8,128)}, f32[256,4096]{1,0:T(8,128)}, s32[]{:T(128)}, s32[]{:T(128)}, /*index=5*/bf16[16,256,128]{2,1,0:T(8,128...) while((s32[]{:T(128)}, f32[256,4096]{1,0:T(8,128)}, f32[256,4096]{1,0:T(8,128)}, ...), condition=%wide.region_3.4_spmd, body=%wide.region_0.3_spmd.sunk | while | flops 272629760 | bytes 17892716 | solution.py:111
  98.2 7.8 %conditional.2 = ((f32[256,4096]{1,0:T(8,128)}, f32[256,4096]{1,0:T(8,128)})) conditional(s32[]{:T(128)} %convert_element_type.30, (f32[256,4096]{1,0:T(8,128)}, f32[256,4096]{1,0:T(8,128)}) %tuple.62, (pred[]{:T(512)}, s32[]{:T(128)}, bf16[16,256,128]{2,1,0:T(8,128)(2,1)S(1)}, s32[]{:T(128)}, bf16[9,128,4096]{2,1,0:T(8,128)(2,1)}, ...), branch_computations={%region_1.1_spmd, %region_2.2_spmd} | conditional | flops 272629760 | bytes 17892492 | solution.py:87
  98.2 7.8 %select_add_fusion = (f32[256,4096]{1,0:T(8,128)}, f32[256,4096]{1,0:T(8,128)}) fusion(f32[256,4096]{1,0:T(8,128)} %get-tuple-element.269, pred[]{:T(512)} %get-tuple-element.270, f32[256,4096]{1,0:T(8,128)} %get-tuple-element.263, pred[]{:T(512)} %get-tuple-element.264, bf16[9,128,4096]{2,1,0:T(8,128)(2,1)} %get-tuple-element.267, s32[]{:T(128)S(6)} %min.21, ...), kind=kOutput, calls=%fused_computation.1 | convolution fusion | flops 272629760 | bytes 17892360 | tf_op jit(solution)/shard_map/while/body/eval_jaxpr/cond/branch_1_fun/dot_general | solution.py:78
  106.1 7.9 %conditional.2 = ((f32[256,4096]{1,0:T(8,128)}, f32[256,4096]{1,0:T(8,128)})) conditional(s32[]{:T(128)} %convert_element_type.30, (f32[256,4096]{1,0:T(8,128)}, f32[256,4096]{1,0:T(8,128)}) %tuple.62, (pred[]{:T(512)}, s32[]{:T(128)}, bf16[16,256,128]{2,1,0:T(8,128)(2,1)S(1)}, s32[]{:T(128)}, bf16[9,128,4096]{2,1,0:T(8,128)(2,1)}, ...), branch_computations={%region_1.1_spmd, %region_2.2_spmd} | conditional | flops 272629760 | bytes 17892492 | solution.py:87
  106.2 7.8 %select_add_fusion = (f32[256,4096]{1,0:T(8,128)}, f32[256,4096]{1,0:T(8,128)}) fusion(f32[256,4096]{1,0:T(8,128)} %get-tuple-element.269, pred[]{:T(512)} %get-tuple-element.270, f32[256,4096]{1,0:T(8,128)} %get-tuple-element.263, pred[]{:T(512)} %get-tuple-element.264, bf16[9,128,4096]{2,1,0:T(8,128)(2,1)} %get-tuple-element.267, s32[]{:T(128)S(6)} %min.21, ...), kind=kOutput, calls=%fused_computation.1 | convolution fusion | flops 272629760 | bytes 17892360 | tf_op jit(solution)/shard_map/while/body/eval_jaxpr/cond/branch_1_fun/dot_general | solution.py:78
  114.0 7.8 %conditional.2 = ((f32[256,4096]{1,0:T(8,128)}, f32[256,4096]{1,0:T(8,128)})) conditional(s32[]{:T(128)} %convert_element_type.30, (f32[256,4096]{1,0:T(8,128)}, f32[256,4096]{1,0:T(8,128)}) %tuple.62, (pred[]{:T(512)}, s32[]{:T(128)}, bf16[16,256,128]{2,1,0:T(8,128)(2,1)S(1)}, s32[]{:T(128)}, bf16[9,128,4096]{2,1,0:T(8,128)(2,1)}, ...), branch_computations={%region_1.1_spmd, %region_2.2_spmd} | conditional | flops 272629760 | bytes 17892492 | solution.py:87
  114.0 7.8 %select_add_fusion = (f32[256,4096]{1,0:T(8,128)}, f32[256,4096]{1,0:T(8,128)}) fusion(f32[256,4096]{1,0:T(8,128)} %get-tuple-element.269, pred[]{:T(512)} %get-tuple-element.270, f32[256,4096]{1,0:T(8,128)} %get-tuple-element.263, pred[]{:T(512)} %get-tuple-element.264, bf16[9,128,4096]{2,1,0:T(8,128)(2,1)} %get-tuple-element.267, s32[]{:T(128)S(6)} %min.21, ...), kind=kOutput, calls=%fused_computation.1 | convolution fusion | flops 272629760 | bytes 17892360 | tf_op jit(solution)/shard_map/while/body/eval_jaxpr/cond/branch_1_fun/dot_general | solution.py:78
  121.8 7.8 %conditional.2 = ((f32[256,4096]{1,0:T(8,128)}, f32[256,4096]{1,0:T(8,128)})) conditional(s32[]{:T(128)} %convert_element_type.30, (f32[256,4096]{1,0:T(8,128)}, f32[256,4096]{1,0:T(8,128)}) %tuple.62, (pred[]{:T(512)}, s32[]{:T(128)}, bf16[16,256,128]{2,1,0:T(8,128)(2,1)S(1)}, s32[]{:T(128)}, bf16[9,128,4096]{2,1,0:T(8,128)(2,1)}, ...), branch_computations={%region_1.1_spmd, %region_2.2_spmd} | conditional | flops 272629760 | bytes 17892492 | solution.py:87
  121.8 7.8 %select_add_fusion = (f32[256,4096]{1,0:T(8,128)}, f32[256,4096]{1,0:T(8,128)}) fusion(f32[256,4096]{1,0:T(8,128)} %get-tuple-element.269, pred[]{:T(512)} %get-tuple-element.270, f32[256,4096]{1,0:T(8,128)} %get-tuple-element.263, pred[]{:T(512)} %get-tuple-element.264, bf16[9,128,4096]{2,1,0:T(8,128)(2,1)} %get-tuple-element.267, s32[]{:T(128)S(6)} %min.21, ...), kind=kOutput, calls=%fused_computation.1 | convolution fusion | flops 272629760 | bytes 17892360 | tf_op jit(solution)/shard_map/while/body/eval_jaxpr/cond/branch_1_fun/dot_general | solution.py:78
  129.7 7.8 %conditional.2 = ((f32[256,4096]{1,0:T(8,128)}, f32[256,4096]{1,0:T(8,128)})) conditional(s32[]{:T(128)} %convert_element_type.30, (f32[256,4096]{1,0:T(8,128)}, f32[256,4096]{1,0:T(8,128)}) %tuple.62, (pred[]{:T(512)}, s32[]{:T(128)}, bf16[16,256,128]{2,1,0:T(8,128)(2,1)S(1)}, s32[]{:T(128)}, bf16[9,128,4096]{2,1,0:T(8,128)(2,1)}, ...), branch_computations={%region_1.1_spmd, %region_2.2_spmd} | conditional | flops 272629760 | bytes 17892492 | solution.py:87
  129.7 7.8 %select_add_fusion = (f32[256,4096]{1,0:T(8,128)}, f32[256,4096]{1,0:T(8,128)}) fusion(f32[256,4096]{1,0:T(8,128)} %get-tuple-element.269, pred[]{:T(512)} %get-tuple-element.270, f32[256,4096]{1,0:T(8,128)} %get-tuple-element.263, pred[]{:T(512)} %get-tuple-element.264, bf16[9,128,4096]{2,1,0:T(8,128)(2,1)} %get-tuple-element.267, s32[]{:T(128)S(6)} %min.21, ...), kind=kOutput, calls=%fused_computation.1 | convolution fusion | flops 272629760 | bytes 17892360 | tf_op jit(solution)/shard_map/while/body/eval_jaxpr/cond/branch_1_fun/dot_general | solution.py:78
  137.5 7.8 %conditional.2 = ((f32[256,4096]{1,0:T(8,128)}, f32[256,4096]{1,0:T(8,128)})) conditional(s32[]{:T(128)} %convert_element_type.30, (f32[256,4096]{1,0:T(8,128)}, f32[256,4096]{1,0:T(8,128)}) %tuple.62, (pred[]{:T(512)}, s32[]{:T(128)}, bf16[16,256,128]{2,1,0:T(8,128)(2,1)S(1)}, s32[]{:T(128)}, bf16[9,128,4096]{2,1,0:T(8,128)(2,1)}, ...), branch_computations={%region_1.1_spmd, %region_2.2_spmd} | conditional | flops 272629760 | bytes 17892492 | solution.py:87
  145.3 7.8 %conditional.2 = ((f32[256,4096]{1,0:T(8,128)}, f32[256,4096]{1,0:T(8,128)})) conditional(s32[]{:T(128)} %convert_element_type.30, (f32[256,4096]{1,0:T(8,128)}, f32[256,4096]{1,0:T(8,128)}) %tuple.62, (pred[]{:T(512)}, s32[]{:T(128)}, bf16[16,256,128]{2,1,0:T(8,128)(2,1)S(1)}, s32[]{:T(128)}, bf16[9,128,4096]{2,1,0:T(8,128)(2,1)}, ...), branch_computations={%region_1.1_spmd, %region_2.2_spmd} | conditional | flops 272629760 | bytes 17892492 | solution.py:87
  145.3 7.8 %select_add_fusion = (f32[256,4096]{1,0:T(8,128)}, f32[256,4096]{1,0:T(8,128)}) fusion(f32[256,4096]{1,0:T(8,128)} %get-tuple-element.269, pred[]{:T(512)} %get-tuple-element.270, f32[256,4096]{1,0:T(8,128)} %get-tuple-element.263, pred[]{:T(512)} %get-tuple-element.264, bf16[9,128,4096]{2,1,0:T(8,128)(2,1)} %get-tuple-element.267, s32[]{:T(128)S(6)} %min.21, ...), kind=kOutput, calls=%fused_computation.1 | convolution fusion | flops 272629760 | bytes 17892360 | tf_op jit(solution)/shard_map/while/body/eval_jaxpr/cond/branch_1_fun/dot_general | solution.py:78
  153.1 7.8 %conditional.2 = ((f32[256,4096]{1,0:T(8,128)}, f32[256,4096]{1,0:T(8,128)})) conditional(s32[]{:T(128)} %convert_element_type.30, (f32[256,4096]{1,0:T(8,128)}, f32[256,4096]{1,0:T(8,128)}) %tuple.62, (pred[]{:T(512)}, s32[]{:T(128)}, bf16[16,256,128]{2,1,0:T(8,128)(2,1)S(1)}, s32[]{:T(128)}, bf16[9,128,4096]{2,1,0:T(8,128)(2,1)}, ...), branch_computations={%region_1.1_spmd, %region_2.2_spmd} | conditional | flops 272629760 | bytes 17892492 | solution.py:87
  161.0 7.8 %conditional.2 = ((f32[256,4096]{1,0:T(8,128)}, f32[256,4096]{1,0:T(8,128)})) conditional(s32[]{:T(128)} %convert_element_type.30, (f32[256,4096]{1,0:T(8,128)}, f32[256,4096]{1,0:T(8,128)}) %tuple.62, (pred[]{:T(512)}, s32[]{:T(128)}, bf16[16,256,128]{2,1,0:T(8,128)(2,1)S(1)}, s32[]{:T(128)}, bf16[9,128,4096]{2,1,0:T(8,128)(2,1)}, ...), branch_computations={%region_1.1_spmd, %region_2.2_spmd} | conditional | flops 272629760 | bytes 17892492 | solution.py:87
  168.9 49.9 %reduce-scatter.9.cloned.1.call-done = f32[256,512]{1,0:T(8,128)} async-done(((f32[256,4096]{1,0:T(8,128)}), f32[256,512]{1,0:T(8,128)}) %reduce-scatter.9.cloned.1.call-update) | async-done | bytes 524304 | tf_op jit(solution)/shard_map/reduce_scatter | solution.py:35
  219.6 18.9 %reduce-scatter.11.cloned.1.call-done = f32[256,256]{1,0:T(8,128)} async-done(((f32[256,512]{1,0:T(8,128)}), f32[256,256]{1,0:T(8,128)}) %reduce-scatter.11.cloned.1.call-update) | async-done | bytes 262160 | tf_op jit(solution)/shard_map/reduce_scatter | solution.py:35
  238.5 60.0 %reduce-scatter.5.cloned.1.call-done = f32[256,512]{1,0:T(8,128)} async-done(((f32[256,4096]{1,0:T(8,128)}), f32[256,512]{1,0:T(8,128)}) %reduce-scatter.5.cloned.1.call-update) | async-done | bytes 524304 | tf_op jit(solution)/shard_map/reduce_scatter | solution.py:35
  345.0 118.1 %all-gather.2.cloned.1.call-done = bf16[512,4096]{1,0:T(8,128)(2,1)} async-done(((bf16[512,256]{1,0:T(8,128)(2,1)}), bf16[512,4096]{1,0:T(8,128)(2,1)}) %all-gather.2.cloned.1.call-update) | async-done | bytes 4194320 | tf_op jit(solution)/shard_map/all_gather | solution.py:45
  465.8 8.8 %fusion.6 = f32[9,256,128]{2,1,0:T(8,128)} fusion(pred[9]{0:T(512)(128)(4,1)S(1)} %iota_compare_fusion, bf16[256,4096]{1,0:T(8,128)(2,1)S(1)} %get-tuple-element.307, bf16[256,4096]{1,0:T(8,128)(2,1)S(1)} %get-tuple-element.306, bf16[1,9,128,4096]{3,2,1,0:T(8,128)(2,1)} %bitcast.41), kind=kOutput, calls=%fused_computation.9 | convolution fusion | flops 2425356288 | bytes 14811145 | tf_op jit(solution)/shard_map/jtd,jfd->jtf/dot_general | solution.py:128
  476.9 37.9 %all_to_all.16 = f32[16,1,256,128]{3,2,1,0:T(8,128)S(1)} all-to-all(f32[16,1,256,128]{3,2,1,0:T(8,128)S(1)} %fusion.12), channel_id=1, replica_groups=mesh['layer'=16,'feat_0'=8,'feat_1'=2] {'layer'}, dimensions={0} | all-to-all | bytes 4194304 | tf_op jit(solution)/shard_map/all_to_all | solution.py:59
  (63 shorter events, 90.8 us)
Async XLA Ops:
  7.2 60.0 %copy-start = (bf16[1,4096,128]{2,1,0:T(8,128)(2,1)S(1)}, bf16[1,4096,128]{2,1,0:T(8,128)(2,1)}, u32[]{:S(2)}) copy-start(bf16[1,4096,128]{2,1,0:T(8,128)(2,1)} %param.12) | copy-start | bytes 3145732
  7.2 60.0 %copy-start.3 = (f32[1,128]{1,0:T(1,128)S(1)}, f32[1,128]{1,0:T(1,128)}, u32[]{:S(2)}) copy-start(f32[1,128]{1,0:T(1,128)} %param.13) | copy-start | bytes 1540
  69.1 24.2 %all-to-all-start.1 = ((bf16[16,1,256,128]{3,2,1,0:T(8,128)(2,1)}), bf16[16,1,256,128]{3,2,1,0:T(8,128)(2,1)S(1)}, u32[]{:S(2)}, u32[]{:S(2)}) async-start(bf16[16,1,256,128]{3,2,1,0:T(8,128)(2,1)} %broadcast_in_dim.69), calls=%async_computation.1 | async-start | bytes 2097152 | tf_op jit(solution)/shard_map/all_to_all | solution.py:19
  75.3 143.5 %reduce-scatter.9.cloned.1.call-start = ((), (), s32[]{:S(2)}) async-start(), calls=%async_computation.9 | async-start | bytes 4718592 | tf_op jit(solution)/shard_map/reduce_scatter | solution.py:35
  168.8 154.4 %copy-start.2 = (bf16[1,256,256]{2,1,0:T(8,128)(2,1)S(1)}, bf16[1,256,256]{2,1,0:T(8,128)(2,1)}, u32[]{:S(2)}) copy-start(bf16[1,256,256]{2,1,0:T(8,128)(2,1)} %param.11) | copy-start | bytes 393220
  168.8 69.7 %reduce-scatter.11.cloned.1.call-start = ((), (), s32[]{:S(2)}) async-start(), calls=%async_computation.10 | async-start | bytes 786432 | tf_op jit(solution)/shard_map/reduce_scatter | solution.py:35
  218.8 79.7 %reduce-scatter.5.cloned.1.call-start = ((), (), s32[]{:S(2)}) async-start(), calls=%async_computation.7 | async-start | bytes 4718592 | tf_op jit(solution)/shard_map/reduce_scatter | solution.py:35
  219.5 99.5 %reduce-scatter.7.cloned.1.call-start = ((), (), s32[]{:S(2)}) async-start(), calls=%async_computation.8 | async-start | bytes 786432 | tf_op jit(solution)/shard_map/reduce_scatter | solution.py:35
  238.5 60.1 %collective-permute-start = (f32[256,256]{1,0:T(8,128)}, f32[256,256]{1,0:T(8,128)S(1)}, u32[]{:S(2)}, u32[]{:S(2)}) collective-permute-start(f32[256,256]{1,0:T(8,128)} %reduce-scatter.11.cloned.1.call-done), channel_id=1, source_target_pairs={{0,16},{16,0},{32,48},{48,32},{64,80},{80,64},{96,112},{112,96},{1... | collective-permute-start | bytes 786440 | tf_op jit(solution)/shard_map/ppermute | solution.py:40
  298.6 164.5 %all-gather.2.cloned.1.call-start = ((), (), s32[]{:S(2)}) async-start(), calls=%async_computation.11 | async-start | bytes 4456448 | tf_op jit(solution)/shard_map/all_gather | solution.py:45
  298.6 9.6 %collective-permute-start.1 = (f32[256,256]{1,0:T(8,128)S(1)}, f32[256,256]{1,0:T(8,128)S(1)}, u32[]{:S(2)}, u32[]{:S(2)}) collective-permute-start(f32[256,256]{1,0:T(8,128)S(1)} %collective-permute-done), channel_id=1, source_target_pairs={{0,32},{16,48},{32,0},{48,16},{64,96},{80,112},{96,64},{112,80},{1... | collective-permute-start | bytes 786440 | tf_op jit(solution)/shard_map/ppermute | solution.py:40
  308.2 7.1 %collective-permute-start.2 = (f32[256,256]{1,0:T(8,128)S(1)}, f32[256,256]{1,0:T(8,128)S(1)}, u32[]{:S(2)}, u32[]{:S(2)}) collective-permute-start(f32[256,256]{1,0:T(8,128)S(1)} %collective-permute-done.1), channel_id=1, source_target_pairs={{0,64},{16,80},{32,96},{48,112},{64,0},{80,16},{96,32},{112,48},{1... | collective-permute-start | bytes 786440 | tf_op jit(solution)/shard_map/ppermute | solution.py:40
  315.3 7.9 %collective-permute-start.3 = (f32[256,256]{1,0:T(8,128)S(1)}, f32[256,256]{1,0:T(8,128)S(1)}, u32[]{:S(2)}, u32[]{:S(2)}) collective-permute-start(f32[256,256]{1,0:T(8,128)S(1)} %collective-permute-done.2), channel_id=1, source_target_pairs={{0,128},{16,144},{32,160},{48,176},{64,192},{80,208},{96,224},{112... | collective-permute-start | bytes 786440 | tf_op jit(solution)/shard_map/ppermute | solution.py:40
  324.2 141.6 %copy-start.1 = (bf16[256,256]{1,0:T(8,128)(2,1)}, bf16[256,256]{1,0:T(8,128)(2,1)S(1)}, u32[]{:S(2)}) copy-start(bf16[256,256]{1,0:T(8,128)(2,1)S(1)} %fusion.16) | copy-start | bytes 393220
  324.2 1.4 collective-permute-start.4
  325.7 7.1 %collective-permute-start.5 = (bf16[256,256]{1,0:T(8,128)(2,1)S(1)}, bf16[256,256]{1,0:T(8,128)(2,1)S(1)}, u32[]{:S(2)}, u32[]{:S(2)}) collective-permute-start(bf16[256,256]{1,0:T(8,128)(2,1)S(1)} %collective-permute-done.4), channel_id=1, source_target_pairs={{0,32},{16,48},{32,0},{48,16},{64,96},{80,112},{96,64},{112,80},{1... | collective-permute-start | bytes 393224 | tf_op jit(solution)/shard_map/ppermute | solution.py:40
  332.7 5.0 collective-permute-start.6
  337.7 6.5 %collective-permute-start.7 = (bf16[256,256]{1,0:T(8,128)(2,1)S(1)}, bf16[256,256]{1,0:T(8,128)(2,1)S(1)}, u32[]{:S(2)}, u32[]{:S(2)}) collective-permute-start(bf16[256,256]{1,0:T(8,128)(2,1)S(1)} %collective-permute-done.6), channel_id=1, source_target_pairs={{0,128},{16,144},{32,160},{48,176},{64,192},{80,208},{96,224},{112... | collective-permute-start | bytes 393224 | tf_op jit(solution)/shard_map/ppermute | solution.py:40
Sparse Core Ops, SparseCore 0:
  168.9 49.7 reduce-scatter.8
  221.3 17.2 reduce-scatter.10
  241.1 57.4 reduce-scatter.4
  300.9 17.2 reduce-scatter.6
  345.0 117.9 all-gather.1
